TPU v7x, 512 devices: a whole 4x8x8 slice. The times are simulated.
512 devices in a mesh: cuts: 32 (over z, y_lo), slab: 16 (over x, y_hi, core).
Axes of the slice: x: 4, y: 8 (y_hi: 2, y_lo: 4; y = y_hi * 4 + y_lo), z: 8, core: 2. Of those that a mesh axis runs over, the one named last changes fastest.
Arguments:
- quasi: bfloat16 [2, 192, 16, 9216], P(None, 'cuts', 'slab'), may hold values from -6 to 6
- counts: int32 [32], replicated, may hold values from 1 to 6, 64 in all
- slot_slice: int32 [192], replicated, may hold values from 0 to 15
- occupation: float32 [192], replicated, may hold values from 0.0078125 to 0.0625
- filter_coef: float32 [16, 9], replicated, may hold values from -2.5 to 2.5
- trap_index: int32 [16, 9216], P('slab'), may hold values from 0 to 31
- trap_table: float32 [32], replicated, may hold values from 0 to 1.5
- mean_field: float32 [16, 9216], P('slab'), may hold values from -1.5 to 0
- pairing: float32 [16, 9216], P('slab'), may hold values from 0.2 to 1
Outputs:
- normal_density: float32 [16, 9216], P('slab', 'cuts')
- anomalous_density: float32 [16, 9216], P('slab', 'cuts')
- new_mean_field: float32 [16, 9216], P('slab', 'cuts')
- new_pairing: float32 [16, 9216], P('slab', 'cuts')
Inputs may be any that keep to these rules, and one draw needn't show every extreme that they name: The live vectors of cut c fill the first counts[c] of its 6 slots; the counts sum to 64 and the largest is exactly 6.
All inputs are finite; a program needn't handle non-finite values.
Results may differ from a plain program's by a relative error of at most 0.0003.
Values may be sent and summed in bfloat16 or wider, within the bound.
No kernel may reach another device: no remote copies, remote signals or barrier semaphores. Data moves between devices by JAX's collectives and lax.ppermute only.
A program may use at most 64 MiB of HBM per device.

v0:
```python
import jax
import jax.numpy as jnp
from jax import lax
from jax.sharding import PartitionSpec as P

NX = 96
VEC_DEV = 2
DEGREE = 8
spectral_scale = 8.5
beta_coef = 0.6
chem_level = 1.0
coupling = 1.0
density_floor = 0.05


def shifted(shard, axis, by):
    devices = lax.axis_size(axis)
    pairs = [(i, i + by) for i in range(devices) if 0 <= i + by < devices]
    return lax.ppermute(shard, axis, pairs)


def combine(field, z_lower, z_upper, y_before, y_after, potential, pairing):
    column = jnp.arange(field.shape[-1]) % NX
    left_ok = (column > 0).astype(jnp.float32)
    right_ok = (column < NX - 1).astype(jnp.float32)
    x_before = jnp.concatenate([jnp.zeros_like(field[..., :1]), field[..., :-1]], axis=3)
    x_after = jnp.concatenate([field[..., 1:], jnp.zeros_like(field[..., :1])], axis=3)
    beside_all = z_lower + z_upper + y_before + y_after
    beside_all = beside_all + x_after * right_ok + x_before * left_ok
    single = 0.5 * (6.0 * field - beside_all) + potential * field
    upper = single[0] + pairing * field[1]
    lower = pairing * field[0] - single[1]
    return jnp.stack([upper, lower]) / spectral_scale


def plane_edges(field):
    below = shifted(field, "slab", 1)
    above = shifted(field, "slab", -1)
    z_lower = jnp.concatenate([below, field[:, :, :-1]], axis=2)
    z_upper = jnp.concatenate([field[:, :, 1:], above], axis=2)
    return (z_lower, z_upper)


def remote_rows(field):
    before = shifted(field[..., -NX:], "cuts", 1)
    after = shifted(field[..., :NX], "cuts", -1)
    y_before = jnp.concatenate([before, field[..., :-NX]], axis=3)
    y_after = jnp.concatenate([field[..., NX:], after], axis=3)
    return (y_before, y_after)


def apply_block(field, potential, pairing, row_source):
    z_lower, z_upper = plane_edges(field)
    y_before, y_after = row_source(field)
    return combine(field, z_lower, z_upper, y_before, y_after, potential, pairing)


def chebyshev(vectors, coefs, operator):
    previous = vectors
    current = operator(vectors)
    filtered = (
        coefs[:, 0][None, :, None, None] * previous + coefs[:, 1][None, :, None, None] * current
    )
    for order in range(2, DEGREE + 1):
        following = 2.0 * operator(current) - previous
        filtered = filtered + coefs[:, order][None, :, None, None] * following
        previous, current = (current, following)
    return filtered


def trap_lookup(index_block, trap_table):
    levels = jnp.arange(trap_table.shape[0])
    onehot = (index_block[:, None, :] == levels[None, :, None]).astype(jnp.float32)
    return jnp.einsum("l,zlf->zf", trap_table, onehot, precision=lax.Precision.HIGHEST)


def slice_coefs(slot_ids, filter_coef):
    levels = jnp.arange(filter_coef.shape[0])
    onehot = (slot_ids[:, None] == levels[None, :]).astype(jnp.float32)
    return jnp.dot(onehot, filter_coef, precision=lax.Precision.HIGHEST)


def body(
    quasi, counts, slot_slice, occupation, filter_coef, trap_index, trap_table, mean_field, pairing
):
    cut_count = lax.axis_size("cuts")
    device = lax.axis_index("cuts")
    cap = quasi.shape[1]
    flat = quasi.shape[3]
    share = flat // cut_count
    offset = device * share
    mean_local = lax.dynamic_slice_in_dim(mean_field, offset, share, 1)
    pairing_local = lax.dynamic_slice_in_dim(pairing, offset, share, 1)
    index_local = lax.dynamic_slice_in_dim(trap_index, offset, share, 1)
    potential = trap_lookup(index_local, trap_table) + mean_local
    moved = lax.all_to_all(quasi, "cuts", split_axis=3, concat_axis=1, tiled=True)
    total_live = VEC_DEV * cut_count
    ends = jnp.cumsum(counts)
    starts = ends - counts
    global_ids = jnp.arange(total_live)
    owner = jnp.sum((ends[None, :] <= global_ids[:, None]).astype(jnp.int32), axis=1)
    owners = jnp.arange(cut_count)
    first = jnp.sum(jnp.where(owners[None, :] == owner[:, None], starts[None, :], 0), axis=1)
    row_ids = owner * cap + global_ids - first
    gathered = jnp.take(moved, row_ids, axis=1).astype(jnp.float32)
    weights = jnp.take(occupation, row_ids)
    coefs = slice_coefs(jnp.take(slot_slice, row_ids), filter_coef)

    def operator(field):
        return apply_block(field, potential, pairing_local, remote_rows)

    filtered = chebyshev(gathered, coefs, operator)
    normal = jnp.sum(weights[:, None, None] * filtered[1] * filtered[1], axis=0)
    anomal = jnp.sum(weights[:, None, None] * filtered[0] * filtered[1], axis=0)
    sums = jnp.stack([normal, anomal])
    normal_density = sums[0]
    anomalous_density = sums[1]
    cube_root = jnp.cbrt(normal_density + density_floor)
    new_mean_field = 0.5 * mean_local + 0.5 * (beta_coef * cube_root * cube_root - chem_level)
    new_pairing = 0.5 * pairing_local - coupling * anomalous_density
    return (normal_density, anomalous_density, new_mean_field, new_pairing)


def solution(mesh):
    return jax.shard_map(
        body,
        mesh=mesh,
        in_specs=(
            P(None, "cuts", "slab", None),
            P(),
            P(),
            P(),
            P(),
            P("slab", None),
            P(),
            P("slab", None),
            P("slab", None),
        ),
        out_specs=(P("slab", "cuts"), P("slab", "cuts"), P("slab", "cuts"), P("slab", "cuts")),
        check_vma=False,
    )
```

profile of v0, /device:TPU:262, one launch (start us, length us, event | category | flops | bytes accessed | tf_op | source)
XLA Modules:
  0.0 266.4 jit_solution(4430877389182085189)
XLA Ops:
  0.7 9.5 %copy.32 = bf16[2,6,1,9216]{1,0,2,3:T(2,128)(2,1)} copy(bf16[2,6,1,9216]{3,0,2,1:T(2,128)(2,1)} %param.9) | data formatting | bytes 442368 | tf_op args[0]
  10.2 11.4 %reshape.1740 = bf16[32,2,1728]{2,1,0:T(2,128)(2,1)} reshape(bf16[9216,1,2,6]{3,2,1,0:T(2,128)(2,1)} %bitcast.79) | data formatting | bytes 442368
  21.6 10.4 %all-to-all-start = ((bf16[32,2,1728]{2,1,0:T(2,128)(2,1)}), bf16[32,2,1728]{2,1,0:T(2,128)(2,1)S(1)}, u32[]{:S(2)}, u32[]{:S(2)}) async-start(bf16[32,2,1728]{2,1,0:T(2,128)(2,1)} %reshape.1740), calls=%async_computation | async-start | bytes 458752 | tf_op jit(solution)/shard_map/all_to_all | solution.py:96
  32.5 0.8 gather_fusion
  33.5 0.8 fusion.67
  34.2 0.8 gather_fusion.1
  35.2 0.9 fusion
  36.1 3.4 %all-to-all-done = bf16[32,2,1728]{2,1,0:T(2,128)(2,1)S(1)} async-done(((bf16[32,2,1728]{2,1,0:T(2,128)(2,1)}), bf16[32,2,1728]{2,1,0:T(2,128)(2,1)S(1)}, u32[]{:S(2)}, u32[]{:S(2)}) %all-to-all-start) | async-done | bytes 221216 | tf_op jit(solution)/shard_map/all_to_all | solution.py:96
  39.6 11.6 %reshape.1741 = bf16[9216,1,2,6]{3,2,1,0:T(2,128)(2,1)} reshape(bf16[32,2,1728]{2,1,0:T(2,128)(2,1)S(1)} %all-to-all-done) | data formatting | bytes 442368
  51.2 8.7 %copy.36 = bf16[2,6,1,32,288]{4,3,0,1,2:T(8,128)(2,1)S(1)} copy(bf16[2,6,1,32,288]{1,0,4,3,2:T(2,128)(2,1)} %bitcast.78) | data formatting | bytes 442368 | tf_op jit(solution)/shard_map/all_to_all | solution.py:96
  60.1 0.8 gather_fusion.2
  61.5 1.9 collective-permute-start
  63.4 8.4 %collective-permute-start.1 = (f32[2,64,1,288]{3,0,1,2:T(2,128)S(1)}, f32[2,64,1,288]{3,0,1,2:T(2,128)S(1)}, u32[]{:S(2)}, u32[]{:S(2)}) collective-permute-start(f32[2,64,1,288]{3,0,1,2:T(2,128)S(1)} %fusion.71), channel_id=1, source_target_pairs={{1,0},{2,1},{3,2},{4,3},{5,4},{6,5},{7,6},{8,7},{9,8},{10,9},{11,1... | collective-permute-start | bytes 442376 | tf_op jit(solution)/shard_map/ppermute | solution.py:19
  71.9 5.5 %collective-permute-start.3 = (f32[2,64,1,96]{3,0,1,2:T(2,128)S(1)}, f32[2,64,1,96]{3,0,1,2:T(2,128)S(1)}, u32[]{:S(2)}, u32[]{:S(2)}) collective-permute-start(f32[2,64,1,96]{3,0,1,2:T(2,128)S(1)} %get-tuple-element.67), channel_id=1, source_target_pairs={{16,0},{32,16},{48,32},{64,48},{80,64},{96,80},{112,96},{128,112},... | collective-permute-start | bytes 147464 | tf_op jit(solution)/shard_map/ppermute | solution.py:19
  77.4 1.9 collective-permute-start.2
  79.5 7.9 %collective-permute-done.2 = f32[2,64,1,96]{3,0,1,2:T(2,128)S(1)} collective-permute-done((f32[2,64,1,96]{3,0,1,2:T(2,128)S(1)}, f32[2,64,1,96]{3,0,1,2:T(2,128)S(1)}, u32[]{:S(2)}, u32[]{:S(2)}) %collective-permute-start.2) | collective-permute-done | bytes 49184 | tf_op jit(solution)/shard_map/ppermute | solution.py:19
  87.5 0.8 multiply_add_fusion.7
  89.1 1.9 collective-permute-start.4
  91.0 8.4 %collective-permute-start.5 = (f32[2,64,1,288]{3,0,1,2:T(2,128)S(1)}, f32[2,64,1,288]{3,0,1,2:T(2,128)S(1)}, u32[]{:S(2)}, u32[]{:S(2)}) collective-permute-start(f32[2,64,1,288]{3,0,1,2:T(2,128)S(1)} %broadcast_multiply_fusion), channel_id=1, source_target_pairs={{1,0},{2,1},{3,2},{4,3},{5,4},{6,5},{7,6},{8,7},{9,8},{10,9},{11,1... | collective-permute-start | bytes 442376 | tf_op jit(solution)/shard_map/ppermute | solution.py:19
  99.5 1.9 collective-permute-start.7
  101.4 3.9 %collective-permute-start.6 = (f32[2,64,1,96]{3,0,1,2:T(2,128)S(1)}, f32[2,64,1,96]{3,0,1,2:T(2,128)S(1)}, u32[]{:S(2)}, u32[]{:S(2)}) collective-permute-start(f32[2,64,1,96]{3,0,1,2:T(2,128)S(1)} %get-tuple-element.60), channel_id=1, source_target_pairs={{0,16},{16,32},{32,48},{48,64},{64,80},{80,96},{96,112},{112,128},... | collective-permute-start | bytes 147464 | tf_op jit(solution)/shard_map/ppermute | solution.py:19
  105.6 5.8 %collective-permute-done.6 = f32[2,64,1,96]{3,0,1,2:T(2,128)S(1)} collective-permute-done((f32[2,64,1,96]{3,0,1,2:T(2,128)S(1)}, f32[2,64,1,96]{3,0,1,2:T(2,128)S(1)}, u32[]{:S(2)}, u32[]{:S(2)}) %collective-permute-start.6) | collective-permute-done | bytes 49184 | tf_op jit(solution)/shard_map/ppermute | solution.py:19
  111.5 0.7 multiply_add_fusion.6
  113.1 1.9 collective-permute-start.8
  115.1 8.4 %collective-permute-start.9 = (f32[2,64,1,288]{3,0,1,2:T(2,128)S(1)}, f32[2,64,1,288]{3,0,1,2:T(2,128)S(1)}, u32[]{:S(2)}, u32[]{:S(2)}) collective-permute-start(f32[2,64,1,288]{3,0,1,2:T(2,128)S(1)} %fusion.9), channel_id=1, source_target_pairs={{1,0},{2,1},{3,2},{4,3},{5,4},{6,5},{7,6},{8,7},{9,8},{10,9},{11,1... | collective-permute-start | bytes 442376 | tf_op jit(solution)/shard_map/ppermute | solution.py:19
  123.5 1.9 collective-permute-start.11
  125.4 4.1 %collective-permute-start.10 = (f32[2,64,1,96]{3,0,1,2:T(2,128)S(1)}, f32[2,64,1,96]{3,0,1,2:T(2,128)S(1)}, u32[]{:S(2)}, u32[]{:S(2)}) collective-permute-start(f32[2,64,1,96]{3,0,1,2:T(2,128)S(1)} %get-tuple-element.54), channel_id=1, source_target_pairs={{0,16},{16,32},{32,48},{48,64},{64,80},{80,96},{96,112},{112,128},... | collective-permute-start | bytes 147464 | tf_op jit(solution)/shard_map/ppermute | solution.py:19
  129.8 0.6 collective-permute-done.11
  130.4 5.3 %collective-permute-done.10 = f32[2,64,1,96]{3,0,1,2:T(2,128)S(1)} collective-permute-done((f32[2,64,1,96]{3,0,1,2:T(2,128)S(1)}, f32[2,64,1,96]{3,0,1,2:T(2,128)S(1)}, u32[]{:S(2)}, u32[]{:S(2)}) %collective-permute-start.10) | collective-permute-done | bytes 49184 | tf_op jit(solution)/shard_map/ppermute | solution.py:19
  135.7 0.9 multiply_add_fusion.5
  137.7 1.9 collective-permute-start.12
  139.6 8.4 %collective-permute-start.13 = (f32[2,64,1,288]{3,0,1,2:T(2,128)S(1)}, f32[2,64,1,288]{3,0,1,2:T(2,128)S(1)}, u32[]{:S(2)}, u32[]{:S(2)}) collective-permute-start(f32[2,64,1,288]{3,0,1,2:T(2,128)S(1)} %fusion.14), channel_id=1, source_target_pairs={{1,0},{2,1},{3,2},{4,3},{5,4},{6,5},{7,6},{8,7},{9,8},{10,9},{11,1... | collective-permute-start | bytes 442376 | tf_op jit(solution)/shard_map/ppermute | solution.py:19
  148.1 1.9 collective-permute-start.15
  150.0 3.9 %collective-permute-start.14 = (f32[2,64,1,96]{3,0,1,2:T(2,128)S(1)}, f32[2,64,1,96]{3,0,1,2:T(2,128)S(1)}, u32[]{:S(2)}, u32[]{:S(2)}) collective-permute-start(f32[2,64,1,96]{3,0,1,2:T(2,128)S(1)} %get-tuple-element.48), channel_id=1, source_target_pairs={{0,16},{16,32},{32,48},{48,64},{64,80},{80,96},{96,112},{112,128},... | collective-permute-start | bytes 147464 | tf_op jit(solution)/shard_map/ppermute | solution.py:19
  154.2 5.8 %collective-permute-done.14 = f32[2,64,1,96]{3,0,1,2:T(2,128)S(1)} collective-permute-done((f32[2,64,1,96]{3,0,1,2:T(2,128)S(1)}, f32[2,64,1,96]{3,0,1,2:T(2,128)S(1)}, u32[]{:S(2)}, u32[]{:S(2)}) %collective-permute-start.14) | collective-permute-done | bytes 49184 | tf_op jit(solution)/shard_map/ppermute | solution.py:19
  160.1 0.9 multiply_add_fusion.4
  162.2 1.9 collective-permute-start.16
  164.1 8.4 %collective-permute-start.17 = (f32[2,64,1,288]{3,0,1,2:T(2,128)S(1)}, f32[2,64,1,288]{3,0,1,2:T(2,128)S(1)}, u32[]{:S(2)}, u32[]{:S(2)}) collective-permute-start(f32[2,64,1,288]{3,0,1,2:T(2,128)S(1)} %fusion.19), channel_id=1, source_target_pairs={{1,0},{2,1},{3,2},{4,3},{5,4},{6,5},{7,6},{8,7},{9,8},{10,9},{11,1... | collective-permute-start | bytes 442376 | tf_op jit(solution)/shard_map/ppermute | solution.py:19
  172.5 1.9 collective-permute-start.19
  174.5 3.9 %collective-permute-start.18 = (f32[2,64,1,96]{3,0,1,2:T(2,128)S(1)}, f32[2,64,1,96]{3,0,1,2:T(2,128)S(1)}, u32[]{:S(2)}, u32[]{:S(2)}) collective-permute-start(f32[2,64,1,96]{3,0,1,2:T(2,128)S(1)} %get-tuple-element.42), channel_id=1, source_target_pairs={{0,16},{16,32},{32,48},{48,64},{64,80},{80,96},{96,112},{112,128},... | collective-permute-start | bytes 147464 | tf_op jit(solution)/shard_map/ppermute | solution.py:19
  178.7 5.8 %collective-permute-done.18 = f32[2,64,1,96]{3,0,1,2:T(2,128)S(1)} collective-permute-done((f32[2,64,1,96]{3,0,1,2:T(2,128)S(1)}, f32[2,64,1,96]{3,0,1,2:T(2,128)S(1)}, u32[]{:S(2)}, u32[]{:S(2)}) %collective-permute-start.18) | collective-permute-done | bytes 49184 | tf_op jit(solution)/shard_map/ppermute | solution.py:19
  184.5 1.1 multiply_add_fusion.3
  186.9 1.9 collective-permute-start.20
  188.9 8.4 %collective-permute-start.21 = (f32[2,64,1,288]{3,0,1,2:T(2,128)S(1)}, f32[2,64,1,288]{3,0,1,2:T(2,128)S(1)}, u32[]{:S(2)}, u32[]{:S(2)}) collective-permute-start(f32[2,64,1,288]{3,0,1,2:T(2,128)S(1)} %fusion.24), channel_id=1, source_target_pairs={{1,0},{2,1},{3,2},{4,3},{5,4},{6,5},{7,6},{8,7},{9,8},{10,9},{11,1... | collective-permute-start | bytes 442376 | tf_op jit(solution)/shard_map/ppermute | solution.py:19
  197.3 1.9 collective-permute-start.23
  199.2 3.9 %collective-permute-start.22 = (f32[2,64,1,96]{3,0,1,2:T(2,128)S(1)}, f32[2,64,1,96]{3,0,1,2:T(2,128)S(1)}, u32[]{:S(2)}, u32[]{:S(2)}) collective-permute-start(f32[2,64,1,96]{3,0,1,2:T(2,128)S(1)} %get-tuple-element.36), channel_id=1, source_target_pairs={{0,16},{16,32},{32,48},{48,64},{64,80},{80,96},{96,112},{112,128},... | collective-permute-start | bytes 147464 | tf_op jit(solution)/shard_map/ppermute | solution.py:19
  203.5 5.9 %collective-permute-done.22 = f32[2,64,1,96]{3,0,1,2:T(2,128)S(1)} collective-permute-done((f32[2,64,1,96]{3,0,1,2:T(2,128)S(1)}, f32[2,64,1,96]{3,0,1,2:T(2,128)S(1)}, u32[]{:S(2)}, u32[]{:S(2)}) %collective-permute-start.22) | collective-permute-done | bytes 49184 | tf_op jit(solution)/shard_map/ppermute | solution.py:19
  209.4 1.1 multiply_add_fusion.2
  210.8 0.7 fusion.29
  211.9 1.9 collective-permute-start.24
  213.8 8.4 %collective-permute-start.25 = (f32[2,64,1,288]{3,0,1,2:T(2,128)S(1)}, f32[2,64,1,288]{3,0,1,2:T(2,128)S(1)}, u32[]{:S(2)}, u32[]{:S(2)}) collective-permute-start(f32[2,64,1,288]{3,0,1,2:T(2,128)S(1)} %fusion.29), channel_id=1, source_target_pairs={{1,0},{2,1},{3,2},{4,3},{5,4},{6,5},{7,6},{8,7},{9,8},{10,9},{11,1... | collective-permute-start | bytes 442376 | tf_op jit(solution)/shard_map/ppermute | solution.py:19
  222.3 1.9 collective-permute-start.27
  224.2 4.1 %collective-permute-start.26 = (f32[2,64,1,96]{3,0,1,2:T(2,128)S(1)}, f32[2,64,1,96]{3,0,1,2:T(2,128)S(1)}, u32[]{:S(2)}, u32[]{:S(2)}) collective-permute-start(f32[2,64,1,96]{3,0,1,2:T(2,128)S(1)} %get-tuple-element.30), channel_id=1, source_target_pairs={{0,16},{16,32},{32,48},{48,64},{64,80},{80,96},{96,112},{112,128},... | collective-permute-start | bytes 147464 | tf_op jit(solution)/shard_map/ppermute | solution.py:19
  228.6 5.8 %collective-permute-done.26 = f32[2,64,1,96]{3,0,1,2:T(2,128)S(1)} collective-permute-done((f32[2,64,1,96]{3,0,1,2:T(2,128)S(1)}, f32[2,64,1,96]{3,0,1,2:T(2,128)S(1)}, u32[]{:S(2)}, u32[]{:S(2)}) %collective-permute-start.26) | collective-permute-done | bytes 49184 | tf_op jit(solution)/shard_map/ppermute | solution.py:19
  234.4 1.3 multiply_add_fusion.1
  235.9 0.8 fusion.34
  237.1 1.9 collective-permute-start.28
  239.0 8.4 %collective-permute-start.29 = (f32[2,64,1,288]{3,0,1,2:T(2,128)S(1)}, f32[2,64,1,288]{3,0,1,2:T(2,128)S(1)}, u32[]{:S(2)}, u32[]{:S(2)}) collective-permute-start(f32[2,64,1,288]{3,0,1,2:T(2,128)S(1)} %fusion.34), channel_id=1, source_target_pairs={{1,0},{2,1},{3,2},{4,3},{5,4},{6,5},{7,6},{8,7},{9,8},{10,9},{11,1... | collective-permute-start | bytes 442376 | tf_op jit(solution)/shard_map/ppermute | solution.py:19
  247.5 1.9 collective-permute-start.31
  249.4 3.9 %collective-permute-start.30 = (f32[2,64,1,96]{3,0,1,2:T(2,128)S(1)}, f32[2,64,1,96]{3,0,1,2:T(2,128)S(1)}, u32[]{:S(2)}, u32[]{:S(2)}) collective-permute-start(f32[2,64,1,96]{3,0,1,2:T(2,128)S(1)} %get-tuple-element.24), channel_id=1, source_target_pairs={{0,16},{16,32},{32,48},{48,64},{64,80},{80,96},{96,112},{112,128},... | collective-permute-start | bytes 147464 | tf_op jit(solution)/shard_map/ppermute | solution.py:19
  253.7 5.8 %collective-permute-done.30 = f32[2,64,1,96]{3,0,1,2:T(2,128)S(1)} collective-permute-done((f32[2,64,1,96]{3,0,1,2:T(2,128)S(1)}, f32[2,64,1,96]{3,0,1,2:T(2,128)S(1)}, u32[]{:S(2)}, u32[]{:S(2)}) %collective-permute-start.30) | collective-permute-done | bytes 49184 | tf_op jit(solution)/shard_map/ppermute | solution.py:19
  259.5 1.3 multiply_add_fusion
  261.1 2.5 fusion.41
  265.0 1.3 multiply_subtract_fusion
  (93 shorter events, 11.8 us)
Async XLA Ops:
  0.6 32.7 %copy-start = (s32[1,9216]{1,0:T(1,128)S(1)}, s32[1,9216]{1,0:T(1,128)}, u32[]{:S(2)}) copy-start(s32[1,9216]{1,0:T(1,128)} %param.14) | copy-start | bytes 110596
  0.6 31.4 %copy-start.3 = (s32[32]{0:T(128)S(1)}, s32[32]{0:T(128)}, u32[]{:S(2)}) copy-start(s32[32]{0:T(128)} %param.10) | copy-start | bytes 388
  0.7 31.9 %copy-start.1 = (f32[192]{0:T(256)S(1)}, f32[192]{0:T(256)}, u32[]{:S(2)}) copy-start(f32[192]{0:T(256)} %param.12) | copy-start | bytes 2308
  0.7 33.6 %copy-start.2 = (s32[192]{0:T(256)S(1)}, s32[192]{0:T(256)}, u32[]{:S(2)}) copy-start(s32[192]{0:T(256)} %param.11) | copy-start | bytes 2308
  0.7 34.4 %copy-start.4 = (f32[16,9]{1,0:T(8,128)S(1)}, f32[16,9]{1,0:T(8,128)}, u32[]{:S(2)}) copy-start(f32[16,9]{1,0:T(8,128)} %param.13) | copy-start | bytes 1732
  0.7 34.6 %copy-start.5 = (f32[32]{0:T(128)S(1)}, f32[32]{0:T(128)}, u32[]{:S(2)}) copy-start(f32[32]{0:T(128)} %param.15) | copy-start | bytes 388
  21.6 18.0 %all-to-all-start = ((bf16[32,2,1728]{2,1,0:T(2,128)(2,1)}), bf16[32,2,1728]{2,1,0:T(2,128)(2,1)S(1)}, u32[]{:S(2)}, u32[]{:S(2)}) async-start(bf16[32,2,1728]{2,1,0:T(2,128)(2,1)} %reshape.1740), calls=%async_computation | async-start | bytes 458752 | tf_op jit(solution)/shard_map/all_to_all | solution.py:96
  61.5 25.9 %collective-permute-start = (f32[2,64,1,288]{3,0,1,2:T(2,128)S(1)}, f32[2,64,1,288]{3,0,1,2:T(2,128)S(1)}, u32[]{:S(2)}, u32[]{:S(2)}) collective-permute-start(f32[2,64,1,288]{3,0,1,2:T(2,128)S(1)} %fusion.71), channel_id=1, source_target_pairs={{0,1},{1,2},{2,3},{3,4},{4,5},{5,6},{6,7},{7,8},{8,9},{9,10},{10,1... | collective-permute-start | bytes 442376 | tf_op jit(solution)/shard_map/ppermute | solution.py:19
  63.4 24.0 %collective-permute-start.1 = (f32[2,64,1,288]{3,0,1,2:T(2,128)S(1)}, f32[2,64,1,288]{3,0,1,2:T(2,128)S(1)}, u32[]{:S(2)}, u32[]{:S(2)}) collective-permute-start(f32[2,64,1,288]{3,0,1,2:T(2,128)S(1)} %fusion.71), channel_id=1, source_target_pairs={{1,0},{2,1},{3,2},{4,3},{5,4},{6,5},{7,6},{8,7},{9,8},{10,9},{11,1... | collective-permute-start | bytes 442376 | tf_op jit(solution)/shard_map/ppermute | solution.py:19
  71.9 7.6 %collective-permute-start.3 = (f32[2,64,1,96]{3,0,1,2:T(2,128)S(1)}, f32[2,64,1,96]{3,0,1,2:T(2,128)S(1)}, u32[]{:S(2)}, u32[]{:S(2)}) collective-permute-start(f32[2,64,1,96]{3,0,1,2:T(2,128)S(1)} %get-tuple-element.67), channel_id=1, source_target_pairs={{16,0},{32,16},{48,32},{64,48},{80,64},{96,80},{112,96},{128,112},... | collective-permute-start | bytes 147464 | tf_op jit(solution)/shard_map/ppermute | solution.py:19
  77.4 10.1 %collective-permute-start.2 = (f32[2,64,1,96]{3,0,1,2:T(2,128)S(1)}, f32[2,64,1,96]{3,0,1,2:T(2,128)S(1)}, u32[]{:S(2)}, u32[]{:S(2)}) collective-permute-start(f32[2,64,1,96]{3,0,1,2:T(2,128)S(1)} %get-tuple-element.66), channel_id=1, source_target_pairs={{0,16},{16,32},{32,48},{48,64},{64,80},{80,96},{96,112},{112,128},... | collective-permute-start | bytes 147464 | tf_op jit(solution)/shard_map/ppermute | solution.py:19
  89.1 22.4 %collective-permute-start.4 = (f32[2,64,1,288]{3,0,1,2:T(2,128)S(1)}, f32[2,64,1,288]{3,0,1,2:T(2,128)S(1)}, u32[]{:S(2)}, u32[]{:S(2)}) collective-permute-start(f32[2,64,1,288]{3,0,1,2:T(2,128)S(1)} %broadcast_multiply_fusion), channel_id=1, source_target_pairs={{0,1},{1,2},{2,3},{3,4},{4,5},{5,6},{6,7},{7,8},{8,9},{9,10},{10,1... | collective-permute-start | bytes 442376 | tf_op jit(solution)/shard_map/ppermute | solution.py:19
  91.0 20.5 %collective-permute-start.5 = (f32[2,64,1,288]{3,0,1,2:T(2,128)S(1)}, f32[2,64,1,288]{3,0,1,2:T(2,128)S(1)}, u32[]{:S(2)}, u32[]{:S(2)}) collective-permute-start(f32[2,64,1,288]{3,0,1,2:T(2,128)S(1)} %broadcast_multiply_fusion), channel_id=1, source_target_pairs={{1,0},{2,1},{3,2},{4,3},{5,4},{6,5},{7,6},{8,7},{9,8},{10,9},{11,1... | collective-permute-start | bytes 442376 | tf_op jit(solution)/shard_map/ppermute | solution.py:19
  99.5 6.2 %collective-permute-start.7 = (f32[2,64,1,96]{3,0,1,2:T(2,128)S(1)}, f32[2,64,1,96]{3,0,1,2:T(2,128)S(1)}, u32[]{:S(2)}, u32[]{:S(2)}) collective-permute-start(f32[2,64,1,96]{3,0,1,2:T(2,128)S(1)} %get-tuple-element.61), channel_id=1, source_target_pairs={{16,0},{32,16},{48,32},{64,48},{80,64},{96,80},{112,96},{128,112},... | collective-permute-start | bytes 147464 | tf_op jit(solution)/shard_map/ppermute | solution.py:19
  101.4 10.1 %collective-permute-start.6 = (f32[2,64,1,96]{3,0,1,2:T(2,128)S(1)}, f32[2,64,1,96]{3,0,1,2:T(2,128)S(1)}, u32[]{:S(2)}, u32[]{:S(2)}) collective-permute-start(f32[2,64,1,96]{3,0,1,2:T(2,128)S(1)} %get-tuple-element.60), channel_id=1, source_target_pairs={{0,16},{16,32},{32,48},{48,64},{64,80},{80,96},{96,112},{112,128},... | collective-permute-start | bytes 147464 | tf_op jit(solution)/shard_map/ppermute | solution.py:19
  113.1 22.6 %collective-permute-start.8 = (f32[2,64,1,288]{3,0,1,2:T(2,128)S(1)}, f32[2,64,1,288]{3,0,1,2:T(2,128)S(1)}, u32[]{:S(2)}, u32[]{:S(2)}) collective-permute-start(f32[2,64,1,288]{3,0,1,2:T(2,128)S(1)} %fusion.9), channel_id=1, source_target_pairs={{0,1},{1,2},{2,3},{3,4},{4,5},{5,6},{6,7},{7,8},{8,9},{9,10},{10,1... | collective-permute-start | bytes 442376 | tf_op jit(solution)/shard_map/ppermute | solution.py:19
  115.1 20.6 %collective-permute-start.9 = (f32[2,64,1,288]{3,0,1,2:T(2,128)S(1)}, f32[2,64,1,288]{3,0,1,2:T(2,128)S(1)}, u32[]{:S(2)}, u32[]{:S(2)}) collective-permute-start(f32[2,64,1,288]{3,0,1,2:T(2,128)S(1)} %fusion.9), channel_id=1, source_target_pairs={{1,0},{2,1},{3,2},{4,3},{5,4},{6,5},{7,6},{8,7},{9,8},{10,9},{11,1... | collective-permute-start | bytes 442376 | tf_op jit(solution)/shard_map/ppermute | solution.py:19
  123.5 6.9 %collective-permute-start.11 = (f32[2,64,1,96]{3,0,1,2:T(2,128)S(1)}, f32[2,64,1,96]{3,0,1,2:T(2,128)S(1)}, u32[]{:S(2)}, u32[]{:S(2)}) collective-permute-start(f32[2,64,1,96]{3,0,1,2:T(2,128)S(1)} %get-tuple-element.55), channel_id=1, source_target_pairs={{16,0},{32,16},{48,32},{64,48},{80,64},{96,80},{112,96},{128,112},... | collective-permute-start | bytes 147464 | tf_op jit(solution)/shard_map/ppermute | solution.py:19
  125.4 10.2 %collective-permute-start.10 = (f32[2,64,1,96]{3,0,1,2:T(2,128)S(1)}, f32[2,64,1,96]{3,0,1,2:T(2,128)S(1)}, u32[]{:S(2)}, u32[]{:S(2)}) collective-permute-start(f32[2,64,1,96]{3,0,1,2:T(2,128)S(1)} %get-tuple-element.54), channel_id=1, source_target_pairs={{0,16},{16,32},{32,48},{48,64},{64,80},{80,96},{96,112},{112,128},... | collective-permute-start | bytes 147464 | tf_op jit(solution)/shard_map/ppermute | solution.py:19
  137.7 22.4 %collective-permute-start.12 = (f32[2,64,1,288]{3,0,1,2:T(2,128)S(1)}, f32[2,64,1,288]{3,0,1,2:T(2,128)S(1)}, u32[]{:S(2)}, u32[]{:S(2)}) collective-permute-start(f32[2,64,1,288]{3,0,1,2:T(2,128)S(1)} %fusion.14), channel_id=1, source_target_pairs={{0,1},{1,2},{2,3},{3,4},{4,5},{5,6},{6,7},{7,8},{8,9},{9,10},{10,1... | collective-permute-start | bytes 442376 | tf_op jit(solution)/shard_map/ppermute | solution.py:19
  139.6 20.5 %collective-permute-start.13 = (f32[2,64,1,288]{3,0,1,2:T(2,128)S(1)}, f32[2,64,1,288]{3,0,1,2:T(2,128)S(1)}, u32[]{:S(2)}, u32[]{:S(2)}) collective-permute-start(f32[2,64,1,288]{3,0,1,2:T(2,128)S(1)} %fusion.14), channel_id=1, source_target_pairs={{1,0},{2,1},{3,2},{4,3},{5,4},{6,5},{7,6},{8,7},{9,8},{10,9},{11,1... | collective-permute-start | bytes 442376 | tf_op jit(solution)/shard_map/ppermute | solution.py:19
  148.1 6.2 %collective-permute-start.15 = (f32[2,64,1,96]{3,0,1,2:T(2,128)S(1)}, f32[2,64,1,96]{3,0,1,2:T(2,128)S(1)}, u32[]{:S(2)}, u32[]{:S(2)}) collective-permute-start(f32[2,64,1,96]{3,0,1,2:T(2,128)S(1)} %get-tuple-element.49), channel_id=1, source_target_pairs={{16,0},{32,16},{48,32},{64,48},{80,64},{96,80},{112,96},{128,112},... | collective-permute-start | bytes 147464 | tf_op jit(solution)/shard_map/ppermute | solution.py:19
  150.0 10.1 %collective-permute-start.14 = (f32[2,64,1,96]{3,0,1,2:T(2,128)S(1)}, f32[2,64,1,96]{3,0,1,2:T(2,128)S(1)}, u32[]{:S(2)}, u32[]{:S(2)}) collective-permute-start(f32[2,64,1,96]{3,0,1,2:T(2,128)S(1)} %get-tuple-element.48), channel_id=1, source_target_pairs={{0,16},{16,32},{32,48},{48,64},{64,80},{80,96},{96,112},{112,128},... | collective-permute-start | bytes 147464 | tf_op jit(solution)/shard_map/ppermute | solution.py:19
  162.2 22.4 %collective-permute-start.16 = (f32[2,64,1,288]{3,0,1,2:T(2,128)S(1)}, f32[2,64,1,288]{3,0,1,2:T(2,128)S(1)}, u32[]{:S(2)}, u32[]{:S(2)}) collective-permute-start(f32[2,64,1,288]{3,0,1,2:T(2,128)S(1)} %fusion.19), channel_id=1, source_target_pairs={{0,1},{1,2},{2,3},{3,4},{4,5},{5,6},{6,7},{7,8},{8,9},{9,10},{10,1... | collective-permute-start | bytes 442376 | tf_op jit(solution)/shard_map/ppermute | solution.py:19
  164.1 20.5 %collective-permute-start.17 = (f32[2,64,1,288]{3,0,1,2:T(2,128)S(1)}, f32[2,64,1,288]{3,0,1,2:T(2,128)S(1)}, u32[]{:S(2)}, u32[]{:S(2)}) collective-permute-start(f32[2,64,1,288]{3,0,1,2:T(2,128)S(1)} %fusion.19), channel_id=1, source_target_pairs={{1,0},{2,1},{3,2},{4,3},{5,4},{6,5},{7,6},{8,7},{9,8},{10,9},{11,1... | collective-permute-start | bytes 442376 | tf_op jit(solution)/shard_map/ppermute | solution.py:19
  172.5 6.2 %collective-permute-start.19 = (f32[2,64,1,96]{3,0,1,2:T(2,128)S(1)}, f32[2,64,1,96]{3,0,1,2:T(2,128)S(1)}, u32[]{:S(2)}, u32[]{:S(2)}) collective-permute-start(f32[2,64,1,96]{3,0,1,2:T(2,128)S(1)} %get-tuple-element.43), channel_id=1, source_target_pairs={{16,0},{32,16},{48,32},{64,48},{80,64},{96,80},{112,96},{128,112},... | collective-permute-start | bytes 147464 | tf_op jit(solution)/shard_map/ppermute | solution.py:19
  174.5 10.1 %collective-permute-start.18 = (f32[2,64,1,96]{3,0,1,2:T(2,128)S(1)}, f32[2,64,1,96]{3,0,1,2:T(2,128)S(1)}, u32[]{:S(2)}, u32[]{:S(2)}) collective-permute-start(f32[2,64,1,96]{3,0,1,2:T(2,128)S(1)} %get-tuple-element.42), channel_id=1, source_target_pairs={{0,16},{16,32},{32,48},{48,64},{64,80},{80,96},{96,112},{112,128},... | collective-permute-start | bytes 147464 | tf_op jit(solution)/shard_map/ppermute | solution.py:19
  186.9 22.5 %collective-permute-start.20 = (f32[2,64,1,288]{3,0,1,2:T(2,128)S(1)}, f32[2,64,1,288]{3,0,1,2:T(2,128)S(1)}, u32[]{:S(2)}, u32[]{:S(2)}) collective-permute-start(f32[2,64,1,288]{3,0,1,2:T(2,128)S(1)} %fusion.24), channel_id=1, source_target_pairs={{0,1},{1,2},{2,3},{3,4},{4,5},{5,6},{6,7},{7,8},{8,9},{9,10},{10,1... | collective-permute-start | bytes 442376 | tf_op jit(solution)/shard_map/ppermute | solution.py:19
  188.9 20.6 %collective-permute-start.21 = (f32[2,64,1,288]{3,0,1,2:T(2,128)S(1)}, f32[2,64,1,288]{3,0,1,2:T(2,128)S(1)}, u32[]{:S(2)}, u32[]{:S(2)}) collective-permute-start(f32[2,64,1,288]{3,0,1,2:T(2,128)S(1)} %fusion.24), channel_id=1, source_target_pairs={{1,0},{2,1},{3,2},{4,3},{5,4},{6,5},{7,6},{8,7},{9,8},{10,9},{11,1... | collective-permute-start | bytes 442376 | tf_op jit(solution)/shard_map/ppermute | solution.py:19
  197.3 6.2 %collective-permute-start.23 = (f32[2,64,1,96]{3,0,1,2:T(2,128)S(1)}, f32[2,64,1,96]{3,0,1,2:T(2,128)S(1)}, u32[]{:S(2)}, u32[]{:S(2)}) collective-permute-start(f32[2,64,1,96]{3,0,1,2:T(2,128)S(1)} %get-tuple-element.37), channel_id=1, source_target_pairs={{16,0},{32,16},{48,32},{64,48},{80,64},{96,80},{112,96},{128,112},... | collective-permute-start | bytes 147464 | tf_op jit(solution)/shard_map/ppermute | solution.py:19
  199.2 10.2 %collective-permute-start.22 = (f32[2,64,1,96]{3,0,1,2:T(2,128)S(1)}, f32[2,64,1,96]{3,0,1,2:T(2,128)S(1)}, u32[]{:S(2)}, u32[]{:S(2)}) collective-permute-start(f32[2,64,1,96]{3,0,1,2:T(2,128)S(1)} %get-tuple-element.36), channel_id=1, source_target_pairs={{0,16},{16,32},{32,48},{48,64},{64,80},{80,96},{96,112},{112,128},... | collective-permute-start | bytes 147464 | tf_op jit(solution)/shard_map/ppermute | solution.py:19
  211.9 22.5 %collective-permute-start.24 = (f32[2,64,1,288]{3,0,1,2:T(2,128)S(1)}, f32[2,64,1,288]{3,0,1,2:T(2,128)S(1)}, u32[]{:S(2)}, u32[]{:S(2)}) collective-permute-start(f32[2,64,1,288]{3,0,1,2:T(2,128)S(1)} %fusion.29), channel_id=1, source_target_pairs={{0,1},{1,2},{2,3},{3,4},{4,5},{5,6},{6,7},{7,8},{8,9},{9,10},{10,1... | collective-permute-start | bytes 442376 | tf_op jit(solution)/shard_map/ppermute | solution.py:19
  213.8 20.6 %collective-permute-start.25 = (f32[2,64,1,288]{3,0,1,2:T(2,128)S(1)}, f32[2,64,1,288]{3,0,1,2:T(2,128)S(1)}, u32[]{:S(2)}, u32[]{:S(2)}) collective-permute-start(f32[2,64,1,288]{3,0,1,2:T(2,128)S(1)} %fusion.29), channel_id=1, source_target_pairs={{1,0},{2,1},{3,2},{4,3},{5,4},{6,5},{7,6},{8,7},{9,8},{10,9},{11,1... | collective-permute-start | bytes 442376 | tf_op jit(solution)/shard_map/ppermute | solution.py:19
  222.3 6.3 %collective-permute-start.27 = (f32[2,64,1,96]{3,0,1,2:T(2,128)S(1)}, f32[2,64,1,96]{3,0,1,2:T(2,128)S(1)}, u32[]{:S(2)}, u32[]{:S(2)}) collective-permute-start(f32[2,64,1,96]{3,0,1,2:T(2,128)S(1)} %get-tuple-element.31), channel_id=1, source_target_pairs={{16,0},{32,16},{48,32},{64,48},{80,64},{96,80},{112,96},{128,112},... | collective-permute-start | bytes 147464 | tf_op jit(solution)/shard_map/ppermute | solution.py:19
  224.2 10.2 %collective-permute-start.26 = (f32[2,64,1,96]{3,0,1,2:T(2,128)S(1)}, f32[2,64,1,96]{3,0,1,2:T(2,128)S(1)}, u32[]{:S(2)}, u32[]{:S(2)}) collective-permute-start(f32[2,64,1,96]{3,0,1,2:T(2,128)S(1)} %get-tuple-element.30), channel_id=1, source_target_pairs={{0,16},{16,32},{32,48},{48,64},{64,80},{80,96},{96,112},{112,128},... | collective-permute-start | bytes 147464 | tf_op jit(solution)/shard_map/ppermute | solution.py:19
  237.1 22.4 %collective-permute-start.28 = (f32[2,64,1,288]{3,0,1,2:T(2,128)S(1)}, f32[2,64,1,288]{3,0,1,2:T(2,128)S(1)}, u32[]{:S(2)}, u32[]{:S(2)}) collective-permute-start(f32[2,64,1,288]{3,0,1,2:T(2,128)S(1)} %fusion.34), channel_id=1, source_target_pairs={{0,1},{1,2},{2,3},{3,4},{4,5},{5,6},{6,7},{7,8},{8,9},{9,10},{10,1... | collective-permute-start | bytes 442376 | tf_op jit(solution)/shard_map/ppermute | solution.py:19
  239.0 20.5 %collective-permute-start.29 = (f32[2,64,1,288]{3,0,1,2:T(2,128)S(1)}, f32[2,64,1,288]{3,0,1,2:T(2,128)S(1)}, u32[]{:S(2)}, u32[]{:S(2)}) collective-permute-start(f32[2,64,1,288]{3,0,1,2:T(2,128)S(1)} %fusion.34), channel_id=1, source_target_pairs={{1,0},{2,1},{3,2},{4,3},{5,4},{6,5},{7,6},{8,7},{9,8},{10,9},{11,1... | collective-permute-start | bytes 442376 | tf_op jit(solution)/shard_map/ppermute | solution.py:19
  247.5 6.2 %collective-permute-start.31 = (f32[2,64,1,96]{3,0,1,2:T(2,128)S(1)}, f32[2,64,1,96]{3,0,1,2:T(2,128)S(1)}, u32[]{:S(2)}, u32[]{:S(2)}) collective-permute-start(f32[2,64,1,96]{3,0,1,2:T(2,128)S(1)} %get-tuple-element.25), channel_id=1, source_target_pairs={{16,0},{32,16},{48,32},{64,48},{80,64},{96,80},{112,96},{128,112},... | collective-permute-start | bytes 147464 | tf_op jit(solution)/shard_map/ppermute | solution.py:19
  249.4 10.1 %collective-permute-start.30 = (f32[2,64,1,96]{3,0,1,2:T(2,128)S(1)}, f32[2,64,1,96]{3,0,1,2:T(2,128)S(1)}, u32[]{:S(2)}, u32[]{:S(2)}) collective-permute-start(f32[2,64,1,96]{3,0,1,2:T(2,128)S(1)} %get-tuple-element.24), channel_id=1, source_target_pairs={{0,16},{16,32},{32,48},{48,64},{64,80},{80,96},{96,112},{112,128},... | collective-permute-start | bytes 147464 | tf_op jit(solution)/shard_map/ppermute | solution.py:19
where the time goes:
time: 268 us; the launch traced here: 266 us
  starting transfers between devices  142 us (53%)
  waiting for transfers between devices  52.9 us (20%)
  local copies, waits for them, and re-layouts  50.7 us (19%)
  other arithmetic  18.3 us (7%)
    ppermute x32, starting transfers between devices, shifted(): return lax.ppermute(shard, axis, pairs)  132 us
    ppermute x32, waiting for transfers between devices, shifted(): return lax.ppermute(shard, axis, pairs)  49.5 us
    unnamed x15, local copies, waits for them, and re-layouts  32.5 us
    all_to_all x1, starting transfers between devices, body(): lax.all_to_all(quasi, 'cuts', split_axis=3, concat_axis=1, tiled=True)  10.4 us
    all_to_all x2, local copies, waits for them, and re-layouts, body(): lax.all_to_all(quasi, 'cuts', split_axis=3, concat_axis=1, tiled=True)  8.98 us
    add x8, other arithmetic, combine(): single = 0.5 * (6.0 * field - beside_all) + potential * field  8.3 us
  transfers between devices with their start and end apart: 33, of which 15 were waited for; matrix products, arithmetic and copies ran while one was open for 2% of the time, Pallas kernels for 0%

commit v1 on v0

--- a/solution.py
+++ b/solution.py
@@ -93,7 +93,10 @@
     pairing_local = lax.dynamic_slice_in_dim(pairing, offset, share, 1)
     index_local = lax.dynamic_slice_in_dim(trap_index, offset, share, 1)
     potential = trap_lookup(index_local, trap_table) + mean_local
-    moved = lax.all_to_all(quasi, "cuts", split_axis=3, concat_axis=1, tiled=True)
+    moved = jnp.concatenate(
+        lax.all_to_all(jnp.stack(jnp.split(quasi, lax.axis_size("cuts"), axis=3)), "cuts", 0, 0),
+        axis=1,
+    )
     total_live = VEC_DEV * cut_count
     ends = jnp.cumsum(counts)
     starts = ends - counts

time: 268 us -> 257 us (0.959)
  the two profiles are of different devices: /device:TPU:262 before, /device:TPU:222 now
where the time goes in v1:
time: 257 us; the launch traced here: 255 us
  starting transfers between devices  141 us (55%)
  waiting for transfers between devices  52.8 us (21%)
  local copies, waits for them, and re-layouts  40.5 us (16%)
  other arithmetic  18.1 us (7%)
    ppermute x32, starting transfers between devices, shifted(): return lax.ppermute(shard, axis, pairs)  130 us
    ppermute x32, waiting for transfers between devices, shifted(): return lax.ppermute(shard, axis, pairs)  49.3 us
    unnamed x45, local copies, waits for them, and re-layouts  30.6 us
    all_to_all x1, starting transfers between devices, body(): lax.all_to_all(jnp.stack(jnp.split(quasi, lax.axis_size('cuts'), axis=3))...  11 us
    add x8, other arithmetic, combine(): single = 0.5 * (6.0 * field - beside_all) + potential * field  8.09 us
  transfers between devices with their start and end apart: 33, of which 15 were waited for; matrix products, arithmetic and copies ran while one was open for 2% of the time, Pallas kernels for 0%

profile of v1, /device:TPU:222, one launch (start us, length us, event | category | flops | bytes accessed | tf_op | source)
XLA Modules:
  0.0 255.1 jit_solution(8898536253630700100)
XLA Ops:
  0.7 1.4 constant_dynamic-update-slice_fusion.31
  2.0 1.4 constant_dynamic-update-slice_fusion.30
  3.4 1.4 constant_dynamic-update-slice_fusion.29
  4.8 1.4 constant_dynamic-update-slice_fusion.28
  6.2 1.3 constant_dynamic-update-slice_fusion.27
  7.5 1.4 constant_dynamic-update-slice_fusion.26
  8.9 1.4 constant_dynamic-update-slice_fusion.25
  10.2 1.4 constant_dynamic-update-slice_fusion.24
  11.6 1.3 constant_dynamic-update-slice_fusion.23
  12.9 1.4 constant_dynamic-update-slice_fusion.22
  14.3 1.4 constant_dynamic-update-slice_fusion.21
  15.7 1.4 constant_dynamic-update-slice_fusion.20
  30.2 11.0 %all-to-all-start = ((bf16[32,2,6,1,288]{4,1,2,3,0:T(2,128)(2,1)}), bf16[32,2,6,1,288]{4,1,2,3,0:T(2,128)(2,1)S(1)}, u32[]{:S(2)}, u32[]{:S(2)}) async-start(bf16[32,2,6,1,288]{4,1,2,3,0:T(2,128)(2,1)} %constant_dynamic-update-slice_fusion), calls=%async_computation | async-start | bytes 589824 | tf_op jit(solution)/shard_map/all_to_all | solution.py:97
  46.1 0.8 fusion
  47.0 3.5 %all-to-all-done = bf16[32,2,6,1,288]{4,1,2,3,0:T(2,128)(2,1)S(1)} async-done(((bf16[32,2,6,1,288]{4,1,2,3,0:T(2,128)(2,1)}), bf16[32,2,6,1,288]{4,1,2,3,0:T(2,128)(2,1)S(1)}, u32[]{:S(2)}, u32[]{:S(2)}) %all-to-all-start) | async-done | bytes 221216 | tf_op jit(solution)/shard_map/all_to_all | solution.py:97
  51.9 1.9 collective-permute-start
  53.8 8.4 %collective-permute-start.1 = (f32[2,64,1,288]{3,0,1,2:T(2,128)S(1)}, f32[2,64,1,288]{3,0,1,2:T(2,128)S(1)}, u32[]{:S(2)}, u32[]{:S(2)}) collective-permute-start(f32[2,64,1,288]{3,0,1,2:T(2,128)S(1)} %fusion.71), channel_id=1, source_target_pairs={{1,0},{2,1},{3,2},{4,3},{5,4},{6,5},{7,6},{8,7},{9,8},{10,9},{11,1... | collective-permute-start | bytes 442376 | tf_op jit(solution)/shard_map/ppermute | solution.py:19
  62.2 4.3 %collective-permute-start.2 = (f32[2,64,1,96]{3,0,1,2:T(2,128)S(1)}, f32[2,64,1,96]{3,0,1,2:T(2,128)S(1)}, u32[]{:S(2)}, u32[]{:S(2)}) collective-permute-start(f32[2,64,1,96]{3,0,1,2:T(2,128)S(1)} %get-tuple-element.66), channel_id=1, source_target_pairs={{0,16},{16,32},{32,48},{48,64},{64,80},{80,96},{96,112},{112,128},... | collective-permute-start | bytes 147464 | tf_op jit(solution)/shard_map/ppermute | solution.py:19
  66.5 1.9 collective-permute-start.3
  68.6 1.4 collective-permute-done.2
  70.0 6.6 %collective-permute-done.3 = f32[2,64,1,96]{3,0,1,2:T(2,128)S(1)} collective-permute-done((f32[2,64,1,96]{3,0,1,2:T(2,128)S(1)}, f32[2,64,1,96]{3,0,1,2:T(2,128)S(1)}, u32[]{:S(2)}, u32[]{:S(2)}) %collective-permute-start.3) | collective-permute-done | bytes 49184 | tf_op jit(solution)/shard_map/ppermute | solution.py:19
  78.2 1.9 collective-permute-start.4
  80.1 8.4 %collective-permute-start.5 = (f32[2,64,1,288]{3,0,1,2:T(2,128)S(1)}, f32[2,64,1,288]{3,0,1,2:T(2,128)S(1)}, u32[]{:S(2)}, u32[]{:S(2)}) collective-permute-start(f32[2,64,1,288]{3,0,1,2:T(2,128)S(1)} %broadcast_multiply_fusion), channel_id=1, source_target_pairs={{1,0},{2,1},{3,2},{4,3},{5,4},{6,5},{7,6},{8,7},{9,8},{10,9},{11,1... | collective-permute-start | bytes 442376 | tf_op jit(solution)/shard_map/ppermute | solution.py:19
  88.6 1.9 collective-permute-start.6
  90.5 3.9 %collective-permute-start.7 = (f32[2,64,1,96]{3,0,1,2:T(2,128)S(1)}, f32[2,64,1,96]{3,0,1,2:T(2,128)S(1)}, u32[]{:S(2)}, u32[]{:S(2)}) collective-permute-start(f32[2,64,1,96]{3,0,1,2:T(2,128)S(1)} %get-tuple-element.61), channel_id=1, source_target_pairs={{16,0},{32,16},{48,32},{64,48},{80,64},{96,80},{112,96},{128,112},... | collective-permute-start | bytes 147464 | tf_op jit(solution)/shard_map/ppermute | solution.py:19
  94.7 5.8 %collective-permute-done.7 = f32[2,64,1,96]{3,0,1,2:T(2,128)S(1)} collective-permute-done((f32[2,64,1,96]{3,0,1,2:T(2,128)S(1)}, f32[2,64,1,96]{3,0,1,2:T(2,128)S(1)}, u32[]{:S(2)}, u32[]{:S(2)}) %collective-permute-start.7) | collective-permute-done | bytes 49184 | tf_op jit(solution)/shard_map/ppermute | solution.py:19
  102.2 1.9 collective-permute-start.8
  104.2 8.4 %collective-permute-start.9 = (f32[2,64,1,288]{3,0,1,2:T(2,128)S(1)}, f32[2,64,1,288]{3,0,1,2:T(2,128)S(1)}, u32[]{:S(2)}, u32[]{:S(2)}) collective-permute-start(f32[2,64,1,288]{3,0,1,2:T(2,128)S(1)} %fusion.9), channel_id=1, source_target_pairs={{1,0},{2,1},{3,2},{4,3},{5,4},{6,5},{7,6},{8,7},{9,8},{10,9},{11,1... | collective-permute-start | bytes 442376 | tf_op jit(solution)/shard_map/ppermute | solution.py:19
  112.6 1.9 collective-permute-start.10
  114.5 3.9 %collective-permute-start.11 = (f32[2,64,1,96]{3,0,1,2:T(2,128)S(1)}, f32[2,64,1,96]{3,0,1,2:T(2,128)S(1)}, u32[]{:S(2)}, u32[]{:S(2)}) collective-permute-start(f32[2,64,1,96]{3,0,1,2:T(2,128)S(1)} %get-tuple-element.55), channel_id=1, source_target_pairs={{16,0},{32,16},{48,32},{64,48},{80,64},{96,80},{112,96},{128,112},... | collective-permute-start | bytes 147464 | tf_op jit(solution)/shard_map/ppermute | solution.py:19
  118.8 5.8 %collective-permute-done.11 = f32[2,64,1,96]{3,0,1,2:T(2,128)S(1)} collective-permute-done((f32[2,64,1,96]{3,0,1,2:T(2,128)S(1)}, f32[2,64,1,96]{3,0,1,2:T(2,128)S(1)}, u32[]{:S(2)}, u32[]{:S(2)}) %collective-permute-start.11) | collective-permute-done | bytes 49184 | tf_op jit(solution)/shard_map/ppermute | solution.py:19
  124.6 0.9 multiply_add_fusion.5
  126.6 1.9 collective-permute-start.12
  128.5 8.4 %collective-permute-start.13 = (f32[2,64,1,288]{3,0,1,2:T(2,128)S(1)}, f32[2,64,1,288]{3,0,1,2:T(2,128)S(1)}, u32[]{:S(2)}, u32[]{:S(2)}) collective-permute-start(f32[2,64,1,288]{3,0,1,2:T(2,128)S(1)} %fusion.14), channel_id=1, source_target_pairs={{1,0},{2,1},{3,2},{4,3},{5,4},{6,5},{7,6},{8,7},{9,8},{10,9},{11,1... | collective-permute-start | bytes 442376 | tf_op jit(solution)/shard_map/ppermute | solution.py:19
  137.0 1.9 collective-permute-start.14
  138.9 4.1 %collective-permute-start.15 = (f32[2,64,1,96]{3,0,1,2:T(2,128)S(1)}, f32[2,64,1,96]{3,0,1,2:T(2,128)S(1)}, u32[]{:S(2)}, u32[]{:S(2)}) collective-permute-start(f32[2,64,1,96]{3,0,1,2:T(2,128)S(1)} %get-tuple-element.49), channel_id=1, source_target_pairs={{16,0},{32,16},{48,32},{64,48},{80,64},{96,80},{112,96},{128,112},... | collective-permute-start | bytes 147464 | tf_op jit(solution)/shard_map/ppermute | solution.py:19
  143.2 5.7 %collective-permute-done.15 = f32[2,64,1,96]{3,0,1,2:T(2,128)S(1)} collective-permute-done((f32[2,64,1,96]{3,0,1,2:T(2,128)S(1)}, f32[2,64,1,96]{3,0,1,2:T(2,128)S(1)}, u32[]{:S(2)}, u32[]{:S(2)}) %collective-permute-start.15) | collective-permute-done | bytes 49184 | tf_op jit(solution)/shard_map/ppermute | solution.py:19
  149.0 0.9 multiply_add_fusion.4
  151.0 1.9 collective-permute-start.16
  152.9 8.4 %collective-permute-start.17 = (f32[2,64,1,288]{3,0,1,2:T(2,128)S(1)}, f32[2,64,1,288]{3,0,1,2:T(2,128)S(1)}, u32[]{:S(2)}, u32[]{:S(2)}) collective-permute-start(f32[2,64,1,288]{3,0,1,2:T(2,128)S(1)} %fusion.19), channel_id=1, source_target_pairs={{1,0},{2,1},{3,2},{4,3},{5,4},{6,5},{7,6},{8,7},{9,8},{10,9},{11,1... | collective-permute-start | bytes 442376 | tf_op jit(solution)/shard_map/ppermute | solution.py:19
  161.4 1.9 collective-permute-start.18
  163.3 3.9 %collective-permute-start.19 = (f32[2,64,1,96]{3,0,1,2:T(2,128)S(1)}, f32[2,64,1,96]{3,0,1,2:T(2,128)S(1)}, u32[]{:S(2)}, u32[]{:S(2)}) collective-permute-start(f32[2,64,1,96]{3,0,1,2:T(2,128)S(1)} %get-tuple-element.43), channel_id=1, source_target_pairs={{16,0},{32,16},{48,32},{64,48},{80,64},{96,80},{112,96},{128,112},... | collective-permute-start | bytes 147464 | tf_op jit(solution)/shard_map/ppermute | solution.py:19
  167.6 5.9 %collective-permute-done.19 = f32[2,64,1,96]{3,0,1,2:T(2,128)S(1)} collective-permute-done((f32[2,64,1,96]{3,0,1,2:T(2,128)S(1)}, f32[2,64,1,96]{3,0,1,2:T(2,128)S(1)}, u32[]{:S(2)}, u32[]{:S(2)}) %collective-permute-start.19) | collective-permute-done | bytes 49184 | tf_op jit(solution)/shard_map/ppermute | solution.py:19
  173.4 1.1 multiply_add_fusion.3
  175.8 1.9 collective-permute-start.20
  177.7 8.4 %collective-permute-start.21 = (f32[2,64,1,288]{3,0,1,2:T(2,128)S(1)}, f32[2,64,1,288]{3,0,1,2:T(2,128)S(1)}, u32[]{:S(2)}, u32[]{:S(2)}) collective-permute-start(f32[2,64,1,288]{3,0,1,2:T(2,128)S(1)} %fusion.24), channel_id=1, source_target_pairs={{1,0},{2,1},{3,2},{4,3},{5,4},{6,5},{7,6},{8,7},{9,8},{10,9},{11,1... | collective-permute-start | bytes 442376 | tf_op jit(solution)/shard_map/ppermute | solution.py:19
  186.2 1.9 collective-permute-start.22
  188.1 3.9 %collective-permute-start.23 = (f32[2,64,1,96]{3,0,1,2:T(2,128)S(1)}, f32[2,64,1,96]{3,0,1,2:T(2,128)S(1)}, u32[]{:S(2)}, u32[]{:S(2)}) collective-permute-start(f32[2,64,1,96]{3,0,1,2:T(2,128)S(1)} %get-tuple-element.37), channel_id=1, source_target_pairs={{16,0},{32,16},{48,32},{64,48},{80,64},{96,80},{112,96},{128,112},... | collective-permute-start | bytes 147464 | tf_op jit(solution)/shard_map/ppermute | solution.py:19
  192.3 5.9 %collective-permute-done.23 = f32[2,64,1,96]{3,0,1,2:T(2,128)S(1)} collective-permute-done((f32[2,64,1,96]{3,0,1,2:T(2,128)S(1)}, f32[2,64,1,96]{3,0,1,2:T(2,128)S(1)}, u32[]{:S(2)}, u32[]{:S(2)}) %collective-permute-start.23) | collective-permute-done | bytes 49184 | tf_op jit(solution)/shard_map/ppermute | solution.py:19
  198.3 1.1 multiply_add_fusion.2
  200.7 1.9 collective-permute-start.24
  202.6 8.4 %collective-permute-start.25 = (f32[2,64,1,288]{3,0,1,2:T(2,128)S(1)}, f32[2,64,1,288]{3,0,1,2:T(2,128)S(1)}, u32[]{:S(2)}, u32[]{:S(2)}) collective-permute-start(f32[2,64,1,288]{3,0,1,2:T(2,128)S(1)} %fusion.29), channel_id=1, source_target_pairs={{1,0},{2,1},{3,2},{4,3},{5,4},{6,5},{7,6},{8,7},{9,8},{10,9},{11,1... | collective-permute-start | bytes 442376 | tf_op jit(solution)/shard_map/ppermute | solution.py:19
  211.1 1.9 collective-permute-start.26
  213.0 3.9 %collective-permute-start.27 = (f32[2,64,1,96]{3,0,1,2:T(2,128)S(1)}, f32[2,64,1,96]{3,0,1,2:T(2,128)S(1)}, u32[]{:S(2)}, u32[]{:S(2)}) collective-permute-start(f32[2,64,1,96]{3,0,1,2:T(2,128)S(1)} %get-tuple-element.31), channel_id=1, source_target_pairs={{16,0},{32,16},{48,32},{64,48},{80,64},{96,80},{112,96},{128,112},... | collective-permute-start | bytes 147464 | tf_op jit(solution)/shard_map/ppermute | solution.py:19
  217.3 5.9 %collective-permute-done.27 = f32[2,64,1,96]{3,0,1,2:T(2,128)S(1)} collective-permute-done((f32[2,64,1,96]{3,0,1,2:T(2,128)S(1)}, f32[2,64,1,96]{3,0,1,2:T(2,128)S(1)}, u32[]{:S(2)}, u32[]{:S(2)}) %collective-permute-start.27) | collective-permute-done | bytes 49184 | tf_op jit(solution)/shard_map/ppermute | solution.py:19
  223.2 1.3 multiply_add_fusion.1
  225.9 1.9 collective-permute-start.28
  227.8 8.4 %collective-permute-start.29 = (f32[2,64,1,288]{3,0,1,2:T(2,128)S(1)}, f32[2,64,1,288]{3,0,1,2:T(2,128)S(1)}, u32[]{:S(2)}, u32[]{:S(2)}) collective-permute-start(f32[2,64,1,288]{3,0,1,2:T(2,128)S(1)} %fusion.34), channel_id=1, source_target_pairs={{1,0},{2,1},{3,2},{4,3},{5,4},{6,5},{7,6},{8,7},{9,8},{10,9},{11,1... | collective-permute-start | bytes 442376 | tf_op jit(solution)/shard_map/ppermute | solution.py:19
  236.3 1.9 collective-permute-start.30
  238.2 4.1 %collective-permute-start.31 = (f32[2,64,1,96]{3,0,1,2:T(2,128)S(1)}, f32[2,64,1,96]{3,0,1,2:T(2,128)S(1)}, u32[]{:S(2)}, u32[]{:S(2)}) collective-permute-start(f32[2,64,1,96]{3,0,1,2:T(2,128)S(1)} %get-tuple-element.25), channel_id=1, source_target_pairs={{16,0},{32,16},{48,32},{64,48},{80,64},{96,80},{112,96},{128,112},... | collective-permute-start | bytes 147464 | tf_op jit(solution)/shard_map/ppermute | solution.py:19
  242.6 5.7 %collective-permute-done.31 = f32[2,64,1,96]{3,0,1,2:T(2,128)S(1)} collective-permute-done((f32[2,64,1,96]{3,0,1,2:T(2,128)S(1)}, f32[2,64,1,96]{3,0,1,2:T(2,128)S(1)}, u32[]{:S(2)}, u32[]{:S(2)}) %collective-permute-start.31) | collective-permute-done | bytes 49184 | tf_op jit(solution)/shard_map/ppermute | solution.py:19
  248.3 1.3 multiply_add_fusion
  249.8 2.5 fusion.41
  253.2 1.3 multiply_subtract_fusion
  (122 shorter events, 32.4 us)
Async XLA Ops:
  0.6 43.2 %copy-start = (s32[1,9216]{1,0:T(1,128)S(1)}, s32[1,9216]{1,0:T(1,128)}, u32[]{:S(2)}) copy-start(s32[1,9216]{1,0:T(1,128)} %param.14) | copy-start | bytes 110596
  0.6 16.4 %copy-start.3 = (bf16[2,6,1,9216]{3,0,2,1:T(2,128)(2,1)S(1)}, bf16[2,6,1,9216]{3,0,2,1:T(2,128)(2,1)}, u32[]{:S(2)}) copy-start(bf16[2,6,1,9216]{3,0,2,1:T(2,128)(2,1)} %param.9) | copy-start | bytes 663556
  30.2 20.3 %all-to-all-start = ((bf16[32,2,6,1,288]{4,1,2,3,0:T(2,128)(2,1)}), bf16[32,2,6,1,288]{4,1,2,3,0:T(2,128)(2,1)S(1)}, u32[]{:S(2)}, u32[]{:S(2)}) async-start(bf16[32,2,6,1,288]{4,1,2,3,0:T(2,128)(2,1)} %constant_dynamic-update-slice_fusion), calls=%async_computation | async-start | bytes 589824 | tf_op jit(solution)/shard_map/all_to_all | solution.py:97
  41.3 0.7 copy-start.4
  42.3 0.7 copy-start.1
  43.8 0.9 copy-start.2
  44.7 0.8 copy-start.5
  45.5 0.7 copy-start.6
  51.9 24.7 %collective-permute-start = (f32[2,64,1,288]{3,0,1,2:T(2,128)S(1)}, f32[2,64,1,288]{3,0,1,2:T(2,128)S(1)}, u32[]{:S(2)}, u32[]{:S(2)}) collective-permute-start(f32[2,64,1,288]{3,0,1,2:T(2,128)S(1)} %fusion.71), channel_id=1, source_target_pairs={{0,1},{1,2},{2,3},{3,4},{4,5},{5,6},{6,7},{7,8},{8,9},{9,10},{10,1... | collective-permute-start | bytes 442376 | tf_op jit(solution)/shard_map/ppermute | solution.py:19
  53.8 22.8 %collective-permute-start.1 = (f32[2,64,1,288]{3,0,1,2:T(2,128)S(1)}, f32[2,64,1,288]{3,0,1,2:T(2,128)S(1)}, u32[]{:S(2)}, u32[]{:S(2)}) collective-permute-start(f32[2,64,1,288]{3,0,1,2:T(2,128)S(1)} %fusion.71), channel_id=1, source_target_pairs={{1,0},{2,1},{3,2},{4,3},{5,4},{6,5},{7,6},{8,7},{9,8},{10,9},{11,1... | collective-permute-start | bytes 442376 | tf_op jit(solution)/shard_map/ppermute | solution.py:19
  62.2 7.8 %collective-permute-start.2 = (f32[2,64,1,96]{3,0,1,2:T(2,128)S(1)}, f32[2,64,1,96]{3,0,1,2:T(2,128)S(1)}, u32[]{:S(2)}, u32[]{:S(2)}) collective-permute-start(f32[2,64,1,96]{3,0,1,2:T(2,128)S(1)} %get-tuple-element.66), channel_id=1, source_target_pairs={{0,16},{16,32},{32,48},{48,64},{64,80},{80,96},{96,112},{112,128},... | collective-permute-start | bytes 147464 | tf_op jit(solution)/shard_map/ppermute | solution.py:19
  66.5 10.1 %collective-permute-start.3 = (f32[2,64,1,96]{3,0,1,2:T(2,128)S(1)}, f32[2,64,1,96]{3,0,1,2:T(2,128)S(1)}, u32[]{:S(2)}, u32[]{:S(2)}) collective-permute-start(f32[2,64,1,96]{3,0,1,2:T(2,128)S(1)} %get-tuple-element.67), channel_id=1, source_target_pairs={{16,0},{32,16},{48,32},{64,48},{80,64},{96,80},{112,96},{128,112},... | collective-permute-start | bytes 147464 | tf_op jit(solution)/shard_map/ppermute | solution.py:19
  78.2 22.4 %collective-permute-start.4 = (f32[2,64,1,288]{3,0,1,2:T(2,128)S(1)}, f32[2,64,1,288]{3,0,1,2:T(2,128)S(1)}, u32[]{:S(2)}, u32[]{:S(2)}) collective-permute-start(f32[2,64,1,288]{3,0,1,2:T(2,128)S(1)} %broadcast_multiply_fusion), channel_id=1, source_target_pairs={{0,1},{1,2},{2,3},{3,4},{4,5},{5,6},{6,7},{7,8},{8,9},{9,10},{10,1... | collective-permute-start | bytes 442376 | tf_op jit(solution)/shard_map/ppermute | solution.py:19
  80.1 20.5 %collective-permute-start.5 = (f32[2,64,1,288]{3,0,1,2:T(2,128)S(1)}, f32[2,64,1,288]{3,0,1,2:T(2,128)S(1)}, u32[]{:S(2)}, u32[]{:S(2)}) collective-permute-start(f32[2,64,1,288]{3,0,1,2:T(2,128)S(1)} %broadcast_multiply_fusion), channel_id=1, source_target_pairs={{1,0},{2,1},{3,2},{4,3},{5,4},{6,5},{7,6},{8,7},{9,8},{10,9},{11,1... | collective-permute-start | bytes 442376 | tf_op jit(solution)/shard_map/ppermute | solution.py:19
  88.6 6.2 %collective-permute-start.6 = (f32[2,64,1,96]{3,0,1,2:T(2,128)S(1)}, f32[2,64,1,96]{3,0,1,2:T(2,128)S(1)}, u32[]{:S(2)}, u32[]{:S(2)}) collective-permute-start(f32[2,64,1,96]{3,0,1,2:T(2,128)S(1)} %get-tuple-element.60), channel_id=1, source_target_pairs={{0,16},{16,32},{32,48},{48,64},{64,80},{80,96},{96,112},{112,128},... | collective-permute-start | bytes 147464 | tf_op jit(solution)/shard_map/ppermute | solution.py:19
  90.5 10.1 %collective-permute-start.7 = (f32[2,64,1,96]{3,0,1,2:T(2,128)S(1)}, f32[2,64,1,96]{3,0,1,2:T(2,128)S(1)}, u32[]{:S(2)}, u32[]{:S(2)}) collective-permute-start(f32[2,64,1,96]{3,0,1,2:T(2,128)S(1)} %get-tuple-element.61), channel_id=1, source_target_pairs={{16,0},{32,16},{48,32},{64,48},{80,64},{96,80},{112,96},{128,112},... | collective-permute-start | bytes 147464 | tf_op jit(solution)/shard_map/ppermute | solution.py:19
  102.2 22.4 %collective-permute-start.8 = (f32[2,64,1,288]{3,0,1,2:T(2,128)S(1)}, f32[2,64,1,288]{3,0,1,2:T(2,128)S(1)}, u32[]{:S(2)}, u32[]{:S(2)}) collective-permute-start(f32[2,64,1,288]{3,0,1,2:T(2,128)S(1)} %fusion.9), channel_id=1, source_target_pairs={{0,1},{1,2},{2,3},{3,4},{4,5},{5,6},{6,7},{7,8},{8,9},{9,10},{10,1... | collective-permute-start | bytes 442376 | tf_op jit(solution)/shard_map/ppermute | solution.py:19
  104.2 20.5 %collective-permute-start.9 = (f32[2,64,1,288]{3,0,1,2:T(2,128)S(1)}, f32[2,64,1,288]{3,0,1,2:T(2,128)S(1)}, u32[]{:S(2)}, u32[]{:S(2)}) collective-permute-start(f32[2,64,1,288]{3,0,1,2:T(2,128)S(1)} %fusion.9), channel_id=1, source_target_pairs={{1,0},{2,1},{3,2},{4,3},{5,4},{6,5},{7,6},{8,7},{9,8},{10,9},{11,1... | collective-permute-start | bytes 442376 | tf_op jit(solution)/shard_map/ppermute | solution.py:19
  112.6 6.2 %collective-permute-start.10 = (f32[2,64,1,96]{3,0,1,2:T(2,128)S(1)}, f32[2,64,1,96]{3,0,1,2:T(2,128)S(1)}, u32[]{:S(2)}, u32[]{:S(2)}) collective-permute-start(f32[2,64,1,96]{3,0,1,2:T(2,128)S(1)} %get-tuple-element.54), channel_id=1, source_target_pairs={{0,16},{16,32},{32,48},{48,64},{64,80},{80,96},{96,112},{112,128},... | collective-permute-start | bytes 147464 | tf_op jit(solution)/shard_map/ppermute | solution.py:19
  114.5 10.1 %collective-permute-start.11 = (f32[2,64,1,96]{3,0,1,2:T(2,128)S(1)}, f32[2,64,1,96]{3,0,1,2:T(2,128)S(1)}, u32[]{:S(2)}, u32[]{:S(2)}) collective-permute-start(f32[2,64,1,96]{3,0,1,2:T(2,128)S(1)} %get-tuple-element.55), channel_id=1, source_target_pairs={{16,0},{32,16},{48,32},{64,48},{80,64},{96,80},{112,96},{128,112},... | collective-permute-start | bytes 147464 | tf_op jit(solution)/shard_map/ppermute | solution.py:19
  126.6 22.4 %collective-permute-start.12 = (f32[2,64,1,288]{3,0,1,2:T(2,128)S(1)}, f32[2,64,1,288]{3,0,1,2:T(2,128)S(1)}, u32[]{:S(2)}, u32[]{:S(2)}) collective-permute-start(f32[2,64,1,288]{3,0,1,2:T(2,128)S(1)} %fusion.14), channel_id=1, source_target_pairs={{0,1},{1,2},{2,3},{3,4},{4,5},{5,6},{6,7},{7,8},{8,9},{9,10},{10,1... | collective-permute-start | bytes 442376 | tf_op jit(solution)/shard_map/ppermute | solution.py:19
  128.5 20.5 %collective-permute-start.13 = (f32[2,64,1,288]{3,0,1,2:T(2,128)S(1)}, f32[2,64,1,288]{3,0,1,2:T(2,128)S(1)}, u32[]{:S(2)}, u32[]{:S(2)}) collective-permute-start(f32[2,64,1,288]{3,0,1,2:T(2,128)S(1)} %fusion.14), channel_id=1, source_target_pairs={{1,0},{2,1},{3,2},{4,3},{5,4},{6,5},{7,6},{8,7},{9,8},{10,9},{11,1... | collective-permute-start | bytes 442376 | tf_op jit(solution)/shard_map/ppermute | solution.py:19
  137.0 6.2 %collective-permute-start.14 = (f32[2,64,1,96]{3,0,1,2:T(2,128)S(1)}, f32[2,64,1,96]{3,0,1,2:T(2,128)S(1)}, u32[]{:S(2)}, u32[]{:S(2)}) collective-permute-start(f32[2,64,1,96]{3,0,1,2:T(2,128)S(1)} %get-tuple-element.48), channel_id=1, source_target_pairs={{0,16},{16,32},{32,48},{48,64},{64,80},{80,96},{96,112},{112,128},... | collective-permute-start | bytes 147464 | tf_op jit(solution)/shard_map/ppermute | solution.py:19
  138.9 10.1 %collective-permute-start.15 = (f32[2,64,1,96]{3,0,1,2:T(2,128)S(1)}, f32[2,64,1,96]{3,0,1,2:T(2,128)S(1)}, u32[]{:S(2)}, u32[]{:S(2)}) collective-permute-start(f32[2,64,1,96]{3,0,1,2:T(2,128)S(1)} %get-tuple-element.49), channel_id=1, source_target_pairs={{16,0},{32,16},{48,32},{64,48},{80,64},{96,80},{112,96},{128,112},... | collective-permute-start | bytes 147464 | tf_op jit(solution)/shard_map/ppermute | solution.py:19
  151.0 22.4 %collective-permute-start.16 = (f32[2,64,1,288]{3,0,1,2:T(2,128)S(1)}, f32[2,64,1,288]{3,0,1,2:T(2,128)S(1)}, u32[]{:S(2)}, u32[]{:S(2)}) collective-permute-start(f32[2,64,1,288]{3,0,1,2:T(2,128)S(1)} %fusion.19), channel_id=1, source_target_pairs={{0,1},{1,2},{2,3},{3,4},{4,5},{5,6},{6,7},{7,8},{8,9},{9,10},{10,1... | collective-permute-start | bytes 442376 | tf_op jit(solution)/shard_map/ppermute | solution.py:19
  152.9 20.5 %collective-permute-start.17 = (f32[2,64,1,288]{3,0,1,2:T(2,128)S(1)}, f32[2,64,1,288]{3,0,1,2:T(2,128)S(1)}, u32[]{:S(2)}, u32[]{:S(2)}) collective-permute-start(f32[2,64,1,288]{3,0,1,2:T(2,128)S(1)} %fusion.19), channel_id=1, source_target_pairs={{1,0},{2,1},{3,2},{4,3},{5,4},{6,5},{7,6},{8,7},{9,8},{10,9},{11,1... | collective-permute-start | bytes 442376 | tf_op jit(solution)/shard_map/ppermute | solution.py:19
  161.4 6.2 %collective-permute-start.18 = (f32[2,64,1,96]{3,0,1,2:T(2,128)S(1)}, f32[2,64,1,96]{3,0,1,2:T(2,128)S(1)}, u32[]{:S(2)}, u32[]{:S(2)}) collective-permute-start(f32[2,64,1,96]{3,0,1,2:T(2,128)S(1)} %get-tuple-element.42), channel_id=1, source_target_pairs={{0,16},{16,32},{32,48},{48,64},{64,80},{80,96},{96,112},{112,128},... | collective-permute-start | bytes 147464 | tf_op jit(solution)/shard_map/ppermute | solution.py:19
  163.3 10.1 %collective-permute-start.19 = (f32[2,64,1,96]{3,0,1,2:T(2,128)S(1)}, f32[2,64,1,96]{3,0,1,2:T(2,128)S(1)}, u32[]{:S(2)}, u32[]{:S(2)}) collective-permute-start(f32[2,64,1,96]{3,0,1,2:T(2,128)S(1)} %get-tuple-element.43), channel_id=1, source_target_pairs={{16,0},{32,16},{48,32},{64,48},{80,64},{96,80},{112,96},{128,112},... | collective-permute-start | bytes 147464 | tf_op jit(solution)/shard_map/ppermute | solution.py:19
  175.8 22.5 %collective-permute-start.20 = (f32[2,64,1,288]{3,0,1,2:T(2,128)S(1)}, f32[2,64,1,288]{3,0,1,2:T(2,128)S(1)}, u32[]{:S(2)}, u32[]{:S(2)}) collective-permute-start(f32[2,64,1,288]{3,0,1,2:T(2,128)S(1)} %fusion.24), channel_id=1, source_target_pairs={{0,1},{1,2},{2,3},{3,4},{4,5},{5,6},{6,7},{7,8},{8,9},{9,10},{10,1... | collective-permute-start | bytes 442376 | tf_op jit(solution)/shard_map/ppermute | solution.py:19
  177.7 20.6 %collective-permute-start.21 = (f32[2,64,1,288]{3,0,1,2:T(2,128)S(1)}, f32[2,64,1,288]{3,0,1,2:T(2,128)S(1)}, u32[]{:S(2)}, u32[]{:S(2)}) collective-permute-start(f32[2,64,1,288]{3,0,1,2:T(2,128)S(1)} %fusion.24), channel_id=1, source_target_pairs={{1,0},{2,1},{3,2},{4,3},{5,4},{6,5},{7,6},{8,7},{9,8},{10,9},{11,1... | collective-permute-start | bytes 442376 | tf_op jit(solution)/shard_map/ppermute | solution.py:19
  186.2 6.2 %collective-permute-start.22 = (f32[2,64,1,96]{3,0,1,2:T(2,128)S(1)}, f32[2,64,1,96]{3,0,1,2:T(2,128)S(1)}, u32[]{:S(2)}, u32[]{:S(2)}) collective-permute-start(f32[2,64,1,96]{3,0,1,2:T(2,128)S(1)} %get-tuple-element.36), channel_id=1, source_target_pairs={{0,16},{16,32},{32,48},{48,64},{64,80},{80,96},{96,112},{112,128},... | collective-permute-start | bytes 147464 | tf_op jit(solution)/shard_map/ppermute | solution.py:19
  188.1 10.2 %collective-permute-start.23 = (f32[2,64,1,96]{3,0,1,2:T(2,128)S(1)}, f32[2,64,1,96]{3,0,1,2:T(2,128)S(1)}, u32[]{:S(2)}, u32[]{:S(2)}) collective-permute-start(f32[2,64,1,96]{3,0,1,2:T(2,128)S(1)} %get-tuple-element.37), channel_id=1, source_target_pairs={{16,0},{32,16},{48,32},{64,48},{80,64},{96,80},{112,96},{128,112},... | collective-permute-start | bytes 147464 | tf_op jit(solution)/shard_map/ppermute | solution.py:19
  200.7 22.5 %collective-permute-start.24 = (f32[2,64,1,288]{3,0,1,2:T(2,128)S(1)}, f32[2,64,1,288]{3,0,1,2:T(2,128)S(1)}, u32[]{:S(2)}, u32[]{:S(2)}) collective-permute-start(f32[2,64,1,288]{3,0,1,2:T(2,128)S(1)} %fusion.29), channel_id=1, source_target_pairs={{0,1},{1,2},{2,3},{3,4},{4,5},{5,6},{6,7},{7,8},{8,9},{9,10},{10,1... | collective-permute-start | bytes 442376 | tf_op jit(solution)/shard_map/ppermute | solution.py:19
  202.6 20.6 %collective-permute-start.25 = (f32[2,64,1,288]{3,0,1,2:T(2,128)S(1)}, f32[2,64,1,288]{3,0,1,2:T(2,128)S(1)}, u32[]{:S(2)}, u32[]{:S(2)}) collective-permute-start(f32[2,64,1,288]{3,0,1,2:T(2,128)S(1)} %fusion.29), channel_id=1, source_target_pairs={{1,0},{2,1},{3,2},{4,3},{5,4},{6,5},{7,6},{8,7},{9,8},{10,9},{11,1... | collective-permute-start | bytes 442376 | tf_op jit(solution)/shard_map/ppermute | solution.py:19
  211.1 6.2 %collective-permute-start.26 = (f32[2,64,1,96]{3,0,1,2:T(2,128)S(1)}, f32[2,64,1,96]{3,0,1,2:T(2,128)S(1)}, u32[]{:S(2)}, u32[]{:S(2)}) collective-permute-start(f32[2,64,1,96]{3,0,1,2:T(2,128)S(1)} %get-tuple-element.30), channel_id=1, source_target_pairs={{0,16},{16,32},{32,48},{48,64},{64,80},{80,96},{96,112},{112,128},... | collective-permute-start | bytes 147464 | tf_op jit(solution)/shard_map/ppermute | solution.py:19
  213.0 10.2 %collective-permute-start.27 = (f32[2,64,1,96]{3,0,1,2:T(2,128)S(1)}, f32[2,64,1,96]{3,0,1,2:T(2,128)S(1)}, u32[]{:S(2)}, u32[]{:S(2)}) collective-permute-start(f32[2,64,1,96]{3,0,1,2:T(2,128)S(1)} %get-tuple-element.31), channel_id=1, source_target_pairs={{16,0},{32,16},{48,32},{64,48},{80,64},{96,80},{112,96},{128,112},... | collective-permute-start | bytes 147464 | tf_op jit(solution)/shard_map/ppermute | solution.py:19
  225.9 22.4 %collective-permute-start.28 = (f32[2,64,1,288]{3,0,1,2:T(2,128)S(1)}, f32[2,64,1,288]{3,0,1,2:T(2,128)S(1)}, u32[]{:S(2)}, u32[]{:S(2)}) collective-permute-start(f32[2,64,1,288]{3,0,1,2:T(2,128)S(1)} %fusion.34), channel_id=1, source_target_pairs={{0,1},{1,2},{2,3},{3,4},{4,5},{5,6},{6,7},{7,8},{8,9},{9,10},{10,1... | collective-permute-start | bytes 442376 | tf_op jit(solution)/shard_map/ppermute | solution.py:19
  227.8 20.5 %collective-permute-start.29 = (f32[2,64,1,288]{3,0,1,2:T(2,128)S(1)}, f32[2,64,1,288]{3,0,1,2:T(2,128)S(1)}, u32[]{:S(2)}, u32[]{:S(2)}) collective-permute-start(f32[2,64,1,288]{3,0,1,2:T(2,128)S(1)} %fusion.34), channel_id=1, source_target_pairs={{1,0},{2,1},{3,2},{4,3},{5,4},{6,5},{7,6},{8,7},{9,8},{10,9},{11,1... | collective-permute-start | bytes 442376 | tf_op jit(solution)/shard_map/ppermute | solution.py:19
  236.3 6.3 %collective-permute-start.30 = (f32[2,64,1,96]{3,0,1,2:T(2,128)S(1)}, f32[2,64,1,96]{3,0,1,2:T(2,128)S(1)}, u32[]{:S(2)}, u32[]{:S(2)}) collective-permute-start(f32[2,64,1,96]{3,0,1,2:T(2,128)S(1)} %get-tuple-element.24), channel_id=1, source_target_pairs={{0,16},{16,32},{32,48},{48,64},{64,80},{80,96},{96,112},{112,128},... | collective-permute-start | bytes 147464 | tf_op jit(solution)/shard_map/ppermute | solution.py:19
  238.2 10.1 %collective-permute-start.31 = (f32[2,64,1,96]{3,0,1,2:T(2,128)S(1)}, f32[2,64,1,96]{3,0,1,2:T(2,128)S(1)}, u32[]{:S(2)}, u32[]{:S(2)}) collective-permute-start(f32[2,64,1,96]{3,0,1,2:T(2,128)S(1)} %get-tuple-element.25), channel_id=1, source_target_pairs={{16,0},{32,16},{48,32},{64,48},{80,64},{96,80},{112,96},{128,112},... | collective-permute-start | bytes 147464 | tf_op jit(solution)/shard_map/ppermute | solution.py:19
